TPU v7x, 32 devices: a whole 2x2x4 slice. The times are simulated.
32 devices in a mesh: row: 8 (over z, y), col: 4 (over x, core).
Axes of the slice: x: 2, y: 2, z: 4, core: 2. Of those that a mesh axis runs over, the one named last changes fastest.
Arguments:
- embeddings: bfloat16 [5, 192, 2048], P(None, None, ('row', 'col')), may hold values from -6 to 6
- scale_weights: float32 [5], replicated, may hold values from 0.1 to 0.5
- vectors: bfloat16 [32, 2048], P(None, ('row', 'col')), may hold values from -6 to 6
Outputs:
- product: float32 [32, 2048], P(None, ('row', 'col'))
All inputs are finite; a program needn't handle non-finite values.
Results may differ from a plain program's by a relative error of at most 0.011.
Values may be sent and summed in bfloat16 or wider, within the bound.
A program may use at most 64 MiB of HBM per device.

v0:
```python
import math
import jax
import jax.numpy as jnp
from jax import lax
from jax.sharding import PartitionSpec as P

SHARP = 3.5


def prepare(embeddings, scale_weights):
    values = embeddings.astype(jnp.float32)
    units = values * lax.rsqrt(jnp.sum(values * values, axis=1, keepdims=True) + 1e-06)
    unit = lax.optimization_barrier(units.astype(jnp.bfloat16))
    weighted = (scale_weights[:, None, None] * unit.astype(jnp.float32)).astype(jnp.bfloat16)
    segments = embeddings.shape[2]
    return (weighted.reshape(-1, segments), unit.reshape(-1, segments))


def tile_terms(row_panel, column_panel, column_vectors, row_ids, column_ids, sharpness):
    cosine = lax.dot_general(
        row_panel, column_panel, (((0,), (0,)), ((), ())), preferred_element_type=jnp.float32
    )
    affinity = jnp.where(
        row_ids[:, None] == column_ids[None, :], jnp.zeros_like(cosine), jnp.exp(sharpness * cosine)
    )
    degree = jnp.sum(affinity, axis=1)
    numerator = lax.dot_general(
        column_vectors,
        affinity.astype(jnp.bfloat16),
        (((1,), (1,)), ((), ())),
        preferred_element_type=jnp.float32,
    )
    return (numerator, degree)


def blocked(row_panel, column_panel, column_vectors, row_ids, column_ids, sharpness):
    width = column_panel.shape[1]
    stride = math.gcd(width, 512)
    numerator = jnp.zeros((column_vectors.shape[0], row_panel.shape[1]), jnp.float32)
    degree = jnp.zeros((row_panel.shape[1],), jnp.float32)
    for offset in range(0, width, stride):
        extra_numerator, extra_degree = tile_terms(
            row_panel,
            column_panel[:, offset : offset + stride],
            column_vectors[:, offset : offset + stride],
            row_ids,
            column_ids[offset : offset + stride],
            sharpness,
        )
        numerator = numerator + extra_numerator
        degree = degree + extra_degree
    return (numerator, degree)


def shards(embeddings, scale_weights, vectors):
    segments = embeddings.shape[2]
    col_count = lax.axis_size("col")
    row_index = lax.axis_index("row")
    col_index = lax.axis_index("col")
    sharpness = SHARP * math.sqrt(embeddings.shape[1])
    weighted, unit = prepare(embeddings, scale_weights)

    def positions_of(panel):
        return jnp.arange(panel.shape[1], dtype=jnp.int32)

    own_panel = lax.all_gather(weighted, "col", axis=1, tiled=True)
    own_ids = row_index * (col_count * segments) + positions_of(own_panel)
    partner_panel, partner_vectors = (
        lax.all_gather(unit, "row", axis=1, tiled=True),
        lax.all_gather(vectors, "row", axis=1, tiled=True),
    )
    positions = positions_of(partner_panel)
    numerator, degree = blocked(
        own_panel,
        partner_panel,
        partner_vectors,
        own_ids,
        (positions // segments * col_count + col_index) * segments + positions % segments,
        sharpness,
    )
    numerator, degree = (
        lax.psum_scatter(numerator, "col", scatter_dimension=1, tiled=True),
        lax.psum_scatter(degree, "col", scatter_dimension=0, tiled=True),
    )
    return numerator / degree[None, :]


def solution(mesh):
    placed = (P(None, None, ("row", "col")), P(), P(None, ("row", "col")))
    return jax.shard_map(
        shards, mesh=mesh, in_specs=placed, out_specs=P(None, ("row", "col")), check_vma=False
    )
```

profile of v0, /device:TPU:0, one launch (start us, length us, event | category | flops | bytes accessed | tf_op | source)
XLA Modules:
  0.0 111.4 jit_solution(14193638312619526555)
XLA Ops:
  6.5 1.1 fusion.2
  7.7 0.1 fusion.3
  7.8 0.1 copy.8
  7.9 0.2 reshape.43
  8.1 34.6 %all_gather.10 = bf16[960,512]{0,1:T(8,128)(2,1)S(1)} all-gather(bf16[960,64]{0,1:T(8,128)(2,1)S(1)} %reshape.43), channel_id=1, replica_groups=mesh['row'=8,'col'=4] {'row'}, dimensions={1}, use_global_device_ids=true | all-gather | bytes 1105920 | tf_op jit(solution)/shard_map/all_gather | solution.py:69
  42.7 0.1 multiply_convert_fusion
  42.8 0.1 copy.7
  42.9 0.2 reshape.42
  43.0 7.2 %all_gather.9 = bf16[960,256]{0,1:T(8,128)(2,1)S(1)} all-gather(bf16[960,64]{0,1:T(8,128)(2,1)S(1)} %reshape.42), channel_id=1, replica_groups=mesh['row'=8,'col'=4] {'col'}, dimensions={1}, use_global_device_ids=true | all-gather | bytes 614400 | tf_op jit(solution)/shard_map/all_gather | solution.py:66
  50.2 0.7 copy-done.1
  50.9 30.5 %all-gather = bf16[8,64,32]{1,2,0:T(8,128)(2,1)S(1)} all-gather(bf16[1,64,32]{1,2,0:T(8,128)(2,1)S(1)} %bitcast.20), channel_id=1, replica_groups=mesh['row'=8,'col'=4] {'row'}, dimensions={0}, use_global_device_ids=true | all-gather | bytes 36864 | tf_op jit(solution)/shard_map/all_gather | solution.py:70
  81.5 0.1 reshape.45
  81.6 0.6 fusion.16
  82.2 0.2 convolution_bitcast_fusion
  82.4 0.7 copy.10
  83.1 0.0 reduce-scatter.4.cloned.1.call-update
  83.1 0.0 copy-start.3
  83.2 0.6 copy-done.3
  83.8 0.6 dynamic-slice
  85.0 5.7 %all-reduce = f32[256]{0:T(256)S(1)} all-reduce(f32[256]{0:T(256)S(1)} %get-tuple-element.5), channel_id=3, replica_groups=mesh['row'=8,'col'=4] {'col'}, use_global_device_ids=true, to_apply=%region_3.4.clone | all-reduce | flops 256 | bytes 2048
  90.7 0.1 dynamic-slice.1
  90.8 12.3 %reduce-scatter.4.cloned.1.call-done = f32[64,32]{1,0:T(8,128)} async-done(((f32[256,32]{1,0:T(8,128)}), f32[64,32]{1,0:T(8,128)}) %reduce-scatter.4.cloned.1.call-update) | async-done | bytes 8208
  103.1 0.8 copy.11
  103.9 0.6 broadcast_divide_fusion
  (10 shorter events, 0.1 us)
Async XLA Ops:
  6.5 1.1 %copy-start = (bf16[5,192,64]{1,2,0:T(8,128)(2,1)S(1)}, bf16[5,192,64]{1,2,0:T(8,128)(2,1)}, u32[]{:S(2)}) copy-start(bf16[5,192,64]{1,2,0:T(8,128)(2,1)} %param.3) | copy-start | bytes 368644
  6.5 96.5 %reduce-scatter.4.cloned.1.call-start = ((), (), s32[]{:S(2)}) async-start(), calls=%async_computation.1 | async-start | bytes 163840
  8.1 34.6 %copy-start.2 = (f32[5]{0:T(128)S(1)}, f32[5]{0:T(128)}, u32[]{:S(2)}) copy-start(f32[5]{0:T(128)} %param.4) | copy-start | bytes 64
  50.2 0.7 copy-start.1
  83.1 0.7 copy-start.3
Sparse Core Ops, SparseCore 0:
  83.3 19.7 reduce-scatter.3
where the time goes:
time: 112 us; the launch traced here: 111 us
  blocking collectives  78 us (70%)
  between operations  14.1 us (13%)
  waiting for transfers between devices  12.3 us (11%)
  local copies, waits for them, and re-layouts  4.23 us (4%)
  other arithmetic  1.94 us (2%)
    all_gather x1, blocking collectives, shards(): lax.all_gather(unit, 'row', axis=1, tiled=True)  34.6 us
    all_gather x1, blocking collectives, shards(): lax.all_gather(vectors, 'row', axis=1, tiled=True)  30.5 us
    unnamed x2, waiting for transfers between devices  12.3 us
    all_gather x1, blocking collectives, shards(): own_panel = lax.all_gather(weighted, 'col', axis=1, tiled=True)  7.17 us
    unnamed x1, blocking collectives  5.67 us
    unnamed x13, local copies, waits for them, and re-layouts  3.68 us
  transfers between devices with their start and end apart: 1, of which 1 were waited for; matrix products, arithmetic and copies ran while one was open for 1% of the time, Pallas kernels for 0%

commit v1 on v0

--- a/solution.py
+++ b/solution.py
@@ -63,7 +63,12 @@
     def positions_of(panel):
         return jnp.arange(panel.shape[1], dtype=jnp.int32)
 
-    own_panel = lax.all_gather(weighted, "col", axis=1, tiled=True)
+    ring = [weighted]
+    for hop in range(3):
+        ring.append(lax.ppermute(ring[-1], "col", [(dev, (dev + 1) % 4) for dev in range(4)]))
+    own_panel = jnp.roll(
+        jnp.concatenate(ring[::-1], axis=1), (lax.axis_index("col") + 1) * ring[0].shape[1], axis=1
+    )
     own_ids = row_index * (col_count * segments) + positions_of(own_panel)
     partner_panel, partner_vectors = (
         lax.all_gather(unit, "row", axis=1, tiled=True),

time: 112 us -> 110 us (0.982)
  blocking collectives: 78 us -> 70.7 us
  waiting for transfers between devices: 12.3 us -> 16.9 us
    all_gather x1 -> x0, blocking collectives: 7.17 us -> none  [shards(): own_panel = lax.all_gather(weighted, 'col', axis=1, tiled=True)]
    ppermute x0 -> x3, waiting for transfers between devices: none -> 4.31 us  [shards(): lax.ppermute(ring[-1], 'col', [(dev, (dev + 1) % 4) for dev in range(4)])]
    unnamed x13 -> x20, local copies, waits for them, and re-layouts: 3.68 us -> 4.26 us
  transfers between devices with their start and end apart: 1 -> 4, of which waited for: 1 -> 2; matrix products, arithmetic and copies ran while one was open for 1% -> 1% of each run, Pallas kernels for 0% -> 0%
where the time goes in v1:
time: 110 us
  blocking collectives  70.7 us (64%)
  waiting for transfers between devices  16.9 us (15%)
  between operations  14.2 us (13%)
  local copies, waits for them, and re-layouts  4.81 us (4%)
  other arithmetic  1.95 us (2%)
    all_gather x1, blocking collectives, shards(): lax.all_gather(unit, 'row', axis=1, tiled=True)  34.5 us
    all_gather x1, blocking collectives, shards(): lax.all_gather(vectors, 'row', axis=1, tiled=True)  30.5 us
    unnamed x2, waiting for transfers between devices  12.6 us
    unnamed x1, blocking collectives  5.67 us
    ppermute x3, waiting for transfers between devices, shards(): lax.ppermute(ring[-1], 'col', [(dev, (dev + 1) % 4) for dev in range(4)])  4.31 us
    unnamed x20, local copies, waits for them, and re-layouts  4.26 us
  transfers between devices with their start and end apart: 4, of which 2 were waited for; matrix products, arithmetic and copies ran while one was open for 1% of the time, Pallas kernels for 0%

profile of v1, /device:TPU:0, one launch (start us, length us, event | category | flops | bytes accessed | tf_op | source)
XLA Modules:
  0.0 109.9 jit_solution(11611013068902548754)
XLA Ops:
  6.5 1.1 %fusion.3 = f32[5,64]{1,0:T(8,128)S(1)} fusion(bf16[5,192,64]{1,2,0:T(8,128)(2,1)} %param.3), kind=kLoop, calls=%fused_computation.7 | loop fusion | flops 184000 | bytes 124160 | tf_op jit(solution)/shard_map/reduce_sum | solution.py:12
  7.7 0.1 fusion.4
  7.8 0.5 copy-done.2
  8.3 0.1 multiply_convert_fusion
  8.4 0.1 copy.7
  8.5 0.2 reshape.42
  8.7 0.5 collective-permute-start
  9.2 0.1 copy.8
  9.3 0.2 reshape.43
  9.5 4.3 %collective-permute-done = bf16[960,64]{0,1:T(8,128)(2,1)S(1)} collective-permute-done((bf16[960,64]{0,1:T(8,128)(2,1)S(1)}, bf16[960,64]{0,1:T(8,128)(2,1)S(1)}, u32[]{:S(2)}, u32[]{:S(2)}) %collective-permute-start) | collective-permute-done | bytes 122912 | tf_op jit(solution)/shard_map/ppermute | solution.py:68
  13.8 34.5 %all_gather.6 = bf16[960,512]{0,1:T(8,128)(2,1)S(1)} all-gather(bf16[960,64]{0,1:T(8,128)(2,1)S(1)} %reshape.43), channel_id=1, replica_groups=mesh['row'=8,'col'=4] {'row'}, dimensions={1}, use_global_device_ids=true | all-gather | bytes 1105920 | tf_op jit(solution)/shard_map/all_gather | solution.py:74
  48.4 0.6 copy-done.1
  49.0 30.5 %all-gather = bf16[8,64,32]{1,2,0:T(8,128)(2,1)S(1)} all-gather(bf16[1,64,32]{1,2,0:T(8,128)(2,1)S(1)} %bitcast.19), channel_id=1, replica_groups=mesh['row'=8,'col'=4] {'row'}, dimensions={0}, use_global_device_ids=true | all-gather | bytes 36864 | tf_op jit(solution)/shard_map/all_gather | solution.py:75
  79.6 0.1 reshape.45
  79.9 0.6 fusion.18
  80.5 0.2 convolution_bitcast_fusion
  80.6 0.8 copy.10
  81.4 0.6 copy-done.3
  82.1 0.6 dynamic-slice
  83.3 5.7 %all-reduce = f32[256]{0:T(256)S(1)} all-reduce(f32[256]{0:T(256)S(1)} %get-tuple-element.5), channel_id=3, replica_groups=mesh['row'=8,'col'=4] {'col'}, use_global_device_ids=true, to_apply=%region_3.4.clone | all-reduce | flops 256 | bytes 2048
  89.0 0.1 dynamic-slice.1
  89.1 12.6 %reduce-scatter.4.cloned.1.call-done = f32[64,32]{1,0:T(8,128)} async-done(((f32[256,32]{1,0:T(8,128)}), f32[64,32]{1,0:T(8,128)}) %reduce-scatter.4.cloned.1.call-update) | async-done | bytes 8208
  101.6 0.8 copy.11
  102.4 0.6 broadcast_divide_fusion
  (23 shorter events, 0.2 us)
Async XLA Ops:
  6.5 1.1 %copy-start = (bf16[5,192,64]{1,2,0:T(8,128)(2,1)S(1)}, bf16[5,192,64]{1,2,0:T(8,128)(2,1)}, u32[]{:S(2)}) copy-start(bf16[5,192,64]{1,2,0:T(8,128)(2,1)} %param.3) | copy-start | bytes 368644
  6.5 95.1 %reduce-scatter.4.cloned.1.call-start = ((), (), s32[]{:S(2)}) async-start(), calls=%async_computation.1 | async-start | bytes 163840
  7.7 0.7 copy-start.2
  8.7 5.1 %collective-permute-start = (bf16[960,64]{0,1:T(8,128)(2,1)S(1)}, bf16[960,64]{0,1:T(8,128)(2,1)S(1)}, u32[]{:S(2)}, u32[]{:S(2)}) collective-permute-start(bf16[960,64]{0,1:T(8,128)(2,1)S(1)} %reshape.42), channel_id=1, source_target_pairs={{0,1},{1,2},{2,3},{3,0},{4,5},{5,6},{6,7},{7,4},{8,9},{9,10},{10,1... | collective-permute-start | bytes 368648 | tf_op jit(solution)/shard_map/ppermute | solution.py:68
  13.8 34.5 %collective-permute-start.1 = (bf16[960,64]{0,1:T(8,128)(2,1)S(1)}, bf16[960,64]{0,1:T(8,128)(2,1)S(1)}, u32[]{:S(2)}, u32[]{:S(2)}) collective-permute-start(bf16[960,64]{0,1:T(8,128)(2,1)S(1)} %collective-permute-done), channel_id=1, source_target_pairs={{0,1},{1,2},{2,3},{3,0},{4,5},{5,6},{6,7},{7,4},{8,9},{9,10},{10,1... | collective-permute-start | bytes 368648 | tf_op jit(solution)/shard_map/ppermute | solution.py:68
  48.3 0.7 copy-start.1
  48.3 31.4 %collective-permute-start.2 = (bf16[960,64]{0,1:T(8,128)(2,1)S(1)}, bf16[960,64]{0,1:T(8,128)(2,1)S(1)}, u32[]{:S(2)}, u32[]{:S(2)}) collective-permute-start(bf16[960,64]{0,1:T(8,128)(2,1)S(1)} %collective-permute-done.1), channel_id=1, source_target_pairs={{0,1},{1,2},{2,3},{3,0},{4,5},{5,6},{6,7},{7,4},{8,9},{9,10},{10,1... | collective-permute-start | bytes 368648 | tf_op jit(solution)/shard_map/ppermute | solution.py:68
  81.4 0.7 copy-start.3
Sparse Core Ops, SparseCore 0:
  81.5 20.0 reduce-scatter.3
